TPU v7x, 32 devices: a whole 2x2x4 slice. The times are simulated.
32 devices in a mesh: flow: 8 (over z, x), leaf: 4 (over y, core).
Axes of the slice: x: 2, y: 2, z: 4, core: 2. Of those that a mesh axis runs over, the one named last changes fastest.
Arguments:
- vel_coef: float32 [81, 16384], P(None, 'flow'), may hold values from -6 to 6
- gp_block: int32 [65536, 1], P(('flow', 'leaf')), may hold values from 0 to 7; in each aligned block of 2048 rows (0 to 2047, 2048 to 4095, ...) at most 512 rows name the same one
- gp_elem: int32 [65536], P(('flow', 'leaf')), may hold values from 0 to 2047
- gp_param: float32 [3, 65536], P(None, ('flow', 'leaf')), may hold values from 0 to 1
- gp_vel: float32 [3, 65536], P(None, ('flow', 'leaf')), may hold values from -6 to 6
- gp_weight: float32 [65536], P(('flow', 'leaf')), may hold values from 0.1 to 1
- gp_pos: float32 [3, 65536], P(None, ('flow', 'leaf')), may hold values from -4 to 4
- contact_patch: int32 [65536], P(('flow', 'leaf')), may hold values from 0 to 1023
- contact_param: float32 [2, 65536], P(None, ('flow', 'leaf')), may hold values from 0 to 1
- patch_ctrl: float32 [27, 8192], P(None, ('flow', 'leaf')), may hold values from -4 to 4
Outputs:
- flow_force: float32 [81, 16384], P(None, ('flow', 'leaf'))
- shell_force: float32 [3, 65536], P(None, ('flow', 'leaf'))
- patch_force: float32 [27, 8192], P(None, ('flow', 'leaf'))
Inputs may be any that keep to these rules, and one draw needn't show every extreme that they name: `gp_block`: the Gauss points of one device lie in at most 512 of each flow block's elements; some block is reached with exactly 512. `contact_patch`: A contact partner is one of the 1024 patches held by the Gauss point's own group, the devices of one index of flow.
All inputs are finite; a program needn't handle non-finite values.
Results may differ from a plain program's by a relative error of at most 0.0001.
Values sent between devices are 32-bit elements; how exact they have to be, the bound alone decides.
No kernel may reach another device: no remote copies, remote signals or barrier semaphores. Data moves between devices by JAX's collectives and lax.ppermute only.
A program may use at most 64 MiB of HBM per device.

v0:
```python
import jax
import jax.numpy as jnp
from jax import lax
from jax.sharding import PartitionSpec as P

BETA = 1.5
STIFF = 2.0
REACH = 0.5


def basis(x):
    return jnp.stack([0.5 * (1.0 - x) ** 2, 0.5 * (1.0 + 2.0 * x - 2.0 * x * x), 0.5 * x * x])


def solid_weights(param):
    first, second, third = (basis(param[0]), basis(param[1]), basis(param[2]))
    return (first[:, None, None, :] * second[None, :, None, :] * third[None, None, :, :]).reshape(
        27, -1
    )


def shell_weights(param):
    first, second = (basis(param[0]), basis(param[1]))
    return (first[:, None, :] * second[None, :, :]).reshape(9, -1)


def contact_force(position, partner_coef, weights):
    near = jnp.sum(partner_coef.reshape(3, 9, -1) * weights[None], axis=1)
    gap = position - near
    return STIFF * gap / (1.0 + jnp.sum(gap * gap, axis=0) / (REACH * REACH))


def decode(block, limit):
    flat = block.reshape(block.shape[0], -1)
    valid = flat[0] >= 0.0
    index = jnp.clip(flat[0].astype(jnp.int32), 0, limit - 1)
    return (flat, valid, index)


def take_columns(source, index):
    return jnp.transpose(jnp.transpose(source)[index])


def add_columns(columns, index, values):
    return jnp.transpose(
        jnp.zeros((columns, values.shape[0]), jnp.float32).at[index].add(jnp.transpose(values))
    )


def sample_flow(coef, index, weights):
    picked = take_columns(coef, index).reshape(3, 27, -1)
    return jnp.sum(picked * weights[None], axis=1)


def spread_rows(columns, index, weights, force):
    terms = (force[:, None, :] * weights[None]).reshape(81, -1)
    return add_columns(columns, index, terms)


def per_device(
    vel_coef,
    gp_block,
    gp_elem,
    gp_param,
    gp_vel,
    gp_weight,
    gp_pos,
    contact_patch,
    contact_param,
    patch_ctrl,
):
    owners = lax.axis_size("flow")
    peers = lax.axis_size("leaf")
    count = gp_elem.shape[0]
    slots_per = 2 * count // owners
    width = slots_per * owners
    elements = vel_coef.shape[1]
    dest = gp_block[:, 0]
    order = jnp.argsort(dest, stable=True)
    sorted_dest = dest[order]
    tally = jnp.sum(
        (dest[:, None] == jnp.arange(owners, dtype=jnp.int32)[None, :]).astype(jnp.int32), axis=0
    )
    starts = jnp.cumsum(tally) - tally
    rank_sorted = jnp.arange(count, dtype=jnp.int32) - starts[sorted_dest]
    slot = jnp.zeros((count,), jnp.int32).at[order].set(rank_sorted * owners + sorted_dest)

    def pack(values, filler):
        buffer = (
            jnp.full((width, values.shape[0]), filler, jnp.float32)
            .at[slot]
            .set(jnp.transpose(values))
        )
        return jnp.transpose(buffer).reshape(values.shape[0], slots_per, owners)

    elem_row = gp_elem.astype(jnp.float32)[None, :]
    payload = pack(jnp.concatenate([elem_row, gp_param, gp_vel, gp_weight[None, :]], axis=0), 0.0)
    occupied = pack(jnp.ones((1, count), jnp.float32), 0.0)
    payload = jnp.concatenate(
        [payload[:1] - (occupied < 0.5).astype(jnp.float32), payload[1:]], axis=0
    )
    block = lax.all_to_all(payload, "flow", split_axis=2, concat_axis=2, tiled=True)
    flat, valid, index = decode(block, elements)
    speed = sample_flow(vel_coef, index, solid_weights(flat[1:4]))
    force = BETA * flat[7][None, :] * (flat[4:7] - speed) * valid[None, :].astype(jnp.float32)
    force = force.reshape(3, block.shape[1], block.shape[2])
    back = lax.all_to_all(force, "flow", split_axis=2, concat_axis=2, tiled=True)
    result = (back, force, block)
    back, arrived, kept = result
    fsi = take_columns(back.reshape(3, width), slot)
    flat, valid, index = decode(kept, elements)
    force = arrived.reshape(3, width) * valid[None, :].astype(jnp.float32)
    piece = lax.all_gather(patch_ctrl, "leaf", axis=1, tiled=True)
    inside = (contact_patch >= 0) & (contact_patch < piece.shape[1])
    taken = take_columns(piece, jnp.clip(contact_patch, 0, piece.shape[1] - 1))
    partner_coef = jnp.where(inside[None, :], taken, jnp.zeros((27, count), jnp.float32))
    shell_w = shell_weights(contact_param)
    pushes = contact_force(gp_pos, partner_coef, shell_w)
    reaction = -(pushes[:, None, :] * shell_w[None]).reshape(27, -1)
    patch_term = add_columns(patch_ctrl.shape[1] * peers, contact_patch, reaction)
    partial_value = spread_rows(elements, index, solid_weights(flat[1:4]), force)
    flow_force, patch_force = (
        lax.psum_scatter(partial_value, "leaf", scatter_dimension=1, tiled=True),
        lax.psum_scatter(patch_term, "leaf", scatter_dimension=1, tiled=True),
    )
    shell_force = pushes - fsi
    return (flow_force, shell_force, patch_force)


def solution(mesh):
    in_specs = (
        P(None, "flow"),
        P(("flow", "leaf"), None),
        P(("flow", "leaf")),
        P(None, ("flow", "leaf")),
        P(None, ("flow", "leaf")),
        P(("flow", "leaf")),
        P(None, ("flow", "leaf")),
        P(("flow", "leaf")),
        P(None, ("flow", "leaf")),
        P(None, ("flow", "leaf")),
    )
    out_specs = (P(None, ("flow", "leaf")), P(None, ("flow", "leaf")), P(None, ("flow", "leaf")))
    return jax.shard_map(
        per_device, mesh=mesh, in_specs=in_specs, out_specs=out_specs, check_vma=False
    )
```

profile of v0, /device:TPU:0, one launch (start us, length us, event | category | flops | bytes accessed | tf_op | source)
XLA Modules:
  0.0 198.3 jit_solution(7097408671395012003)
XLA Ops:
  7.2 0.9 convert_reduce_fusion
  8.1 0.2 reduce-window.9
  8.3 0.7 fusion.28
  9.0 5.7 %sort.17 = (s32[2048]{0:T(1024)}, s32[2048]{0:T(1024)S(1)}) sort(s32[2048]{0:T(1024)} %bitcast.41, s32[2048]{0:T(1024)S(1)} %iota.11), dimensions={0}, to_apply=%region_0.0 | sort | flops 22528 | bytes 32768 | tf_op jit(solution)/shard_map/jit(argsort)/sort | solution.py:79
  14.8 11.8 %gather_fusion = s32[2048]{0:T(1024)S(1)} fusion(s32[2048]{0:T(1024)S(1)} %bitcast.42, s32[2048]{0:T(1024)S(1)} %get-tuple-element.53), kind=kCustom, calls=%fused_computation | custom fusion | bytes 24576 | tf_op jit(solution)/shard_map/gather | solution.py:80
  26.6 4.4 %compare_select_fusion.2 = s32[2048,1]{0,1:T(1,128)S(1)} fusion(s32[]{:T(128)} %bitcast.5, s32[]{:T(128)} %bitcast.6, s32[]{:T(128)} %bitcast.7, s32[]{:T(128)} %bitcast.8, s32[]{:T(128)} %bitcast.9, s32[]{:T(128)} %bitcast.11, s32[]{:T(128)} %bitcast.10, s32[2048,1]{0,1:T(1,128)S(1)} %bitcast.54), kind=kLoop, calls=%fused_computation.44 | loop fusion | flops 30720 | bytes 16412 | tf_op jit(solution)/shard_map/gather | solution.py:85
  31.0 0.7 fusion.22
  31.7 8.0 %scatter_custom_fusion = s32[2048]{0:T(1024)S(1)} fusion(s32[2048]{0:T(1024)S(1)} %get-tuple-element.54, s32[2048]{0:T(1024)S(1)} %fusion.22, s32[]{:T(128)} %constant.14.clone.1), kind=kCustom, calls=%fused_computation.99 | custom fusion | bytes 8196 | tf_op jit(solution)/shard_map/scatter | solution.py:86
  39.7 0.6 broadcast_clamp_fusion.1
  40.4 0.3 copy.139
  40.7 6.1 %scatter_custom_fusion.1 = f32[4096,8]{1,0:T(8,128)S(1)} fusion(s32[2048]{0:T(1024)S(1)} %get-tuple-element.52, f32[2048,8]{1,0:T(8,128)S(1)} %copy.139, f32[]{:T(128)} %constant.13.clone.1), kind=kCustom, calls=%fused_computation.13 | custom fusion | bytes 131076 | tf_op jit(solution)/shard_map/scatter | solution.py:92
  46.8 0.6 slice_reduce_fusion
  47.5 2.0 slice_bitcast_fusion
  49.6 8.1 %scatter_custom_fusion.2 = f32[4096]{0:T(1024)S(1)} fusion(s32[2048]{0:T(1024)S(1)} %get-tuple-element.52, f32[2048]{0:T(1024)S(1)} %broadcast.365, f32[]{:T(128)} %constant.13.clone.1), kind=kCustom, calls=%fused_computation.88 | custom fusion | bytes 16388 | tf_op jit(solution)/shard_map/scatter | solution.py:92
  58.0 2.2 %copy.141 = f32[7,512,8]{1,0,2:T(8,128)S(1)} copy(f32[7,512,8]{0,2,1:T(8,128)} %slice_bitcast_fusion) | data formatting | bytes 229376 | tf_op jit(solution)/shard_map/slice | solution.py:100
  60.2 0.7 pad_maximum_fusion
  60.9 7.3 %all-to-all-start = ((f32[8,512,8]{1,0,2:T(8,128)}), f32[8,512,8]{1,0,2:T(8,128)S(1)}, u32[]{:S(2)}, u32[]{:S(2)}) async-start(f32[8,512,8]{1,0,2:T(8,128)} %pad_maximum_fusion), calls=%async_computation | async-start | bytes 262144 | tf_op jit(solution)/shard_map/all_to_all | solution.py:102
  68.2 0.6 compare_select_fusion.8
  69.1 7.4 %all_gather.3 = f32[27,1024]{0,1:T(8,128)S(1)} all-gather(f32[27,256]{0,1:T(8,128)S(1)} %copy.155), channel_id=1, replica_groups=mesh['flow'=8,'leaf'=4] {'leaf'}, dimensions={1}, use_global_device_ids=true | all-gather | bytes 138240 | tf_op jit(solution)/shard_map/all_gather | solution.py:113
  76.5 5.5 %gather_fusion.2 = f32[2048,27]{1,0:T(8,128)S(1)} fusion(f32[1024,27]{1,0:T(8,128)S(1)} %bitcast.44, s32[2048]{0:T(1024)S(1)} %get-tuple-element.50), kind=kCustom, calls=%fused_computation.2 | custom fusion | bytes 450560 | tf_op jit(solution)/shard_map/gather | solution.py:41
  82.0 0.3 select_bitcast_fusion
  82.4 0.3 copy.156
  82.9 0.2 copy-done.2
  83.1 0.3 copy.148
  83.5 0.6 multiply_add_fusion.5
  85.6 1.0 mul.473
  87.0 10.8 %gather_fusion.1 = f32[4096,81]{1,0:T(8,128)S(1)} fusion(f32[2048,81]{1,0:T(8,128)S(1)} %bitcast.43, s32[4096]{0:T(1024)S(1)} %broadcast_clamp_fusion), kind=kCustom, calls=%fused_computation.1 | custom fusion | bytes 2670592 | tf_op jit(solution)/shard_map/gather | solution.py:41
  97.8 1.8 copy.149
  99.5 1.6 reshape.456
  101.1 0.2 multiply_reduce_fusion
  101.4 0.4 reduce_sum.42
  101.8 0.2 copy.157
  102.1 0.3 copy.147
  102.4 0.7 copy.158
  103.1 6.0 %all-to-all-start.1 = ((f32[3,512,8]{1,0,2:T(4,128)}), f32[3,512,8]{1,0,2:T(4,128)S(1)}, u32[]{:S(2)}, u32[]{:S(2)}) async-start(f32[3,512,8]{1,0,2:T(4,128)} %copy.158), calls=%async_computation.2 | async-start | bytes 131072 | tf_op jit(solution)/shard_map/all_to_all | solution.py:107
  109.1 0.4 slice.63
  110.2 5.8 %all-to-all-done.1 = f32[3,512,8]{1,0,2:T(4,128)S(1)} async-done(((f32[3,512,8]{1,0,2:T(4,128)}), f32[3,512,8]{1,0,2:T(4,128)S(1)}, u32[]{:S(2)}, u32[]{:S(2)}) %all-to-all-start.1) | async-done | bytes 49184 | tf_op jit(solution)/shard_map/all_to_all | solution.py:107
  116.0 0.8 copy.159
  116.8 7.6 %gather_fusion.3 = f32[2048,3]{1,0:T(8,128)} fusion(f32[4096,3]{1,0:T(8,128)S(1)} %bitcast.45, s32[2048]{0:T(1024)S(1)} %copy-done.9), kind=kCustom, calls=%fused_computation.3 | custom fusion | bytes 57344 | tf_op jit(solution)/shard_map/gather | solution.py:41
  124.4 1.6 copy.160
  125.9 0.6 bitcast_subtract_fusion
  126.7 0.4 copy.161
  127.0 12.4 %scatter_custom_fusion.4 = f32[1024,27]{1,0:T(8,128)} fusion(s32[2048]{0:T(1024)} %get-tuple-element.49, f32[2048,27]{1,0:T(8,128)S(1)} %copy.161, f32[]{:T(128)} %constant.13.clone.1), kind=kCustom, calls=%fused_computation.21 | custom fusion | flops 55296 | bytes 111104 | tf_op jit(solution)/shard_map/scatter-add | solution.py:46
  139.8 0.8 copy.154
  140.7 23.4 %scatter_custom_fusion.3 = f32[2048,81]{1,0:T(8,128)} fusion(s32[4096]{0:T(1024)S(1)} %bitcast.56, f32[4096,81]{1,0:T(8,128)S(1)} %copy.154, f32[]{:T(128)} %constant.13.clone.1), kind=kCustom, calls=%fused_computation.16 | custom fusion | flops 331776 | bytes 663556 | tf_op jit(solution)/shard_map/scatter-add | solution.py:46
  164.1 1.6 copy.163
  165.7 24.0 %reduce-scatter.3.cloned.1.call-done = f32[81,512]{0,1:T(8,128)} async-done(((f32[81,2048]{0,1:T(8,128)}), f32[81,512]{0,1:T(8,128)}) %reduce-scatter.3.cloned.1.call-update) | async-done | bytes 165904 | tf_op jit(solution)/shard_map/reduce_scatter | solution.py:123
  189.7 1.8 copy.162
  (84 shorter events, 3.9 us)
Async XLA Ops:
  7.2 7.5 %copy-start = (s32[2048,1]{0,1:T(1,128)S(1)}, s32[2048,1]{0,1:T(1,128)}, u32[]{:S(2)}) copy-start(s32[2048,1]{0,1:T(1,128)} %param.11) | copy-start | bytes 24580
  14.7 25.6 %copy-start.12 = (s32[2048]{0:T(1024)S(1)}, s32[2048]{0:T(1024)}, u32[]{:S(2)}) copy-start(s32[2048]{0:T(1024)} %param.12) | copy-start | bytes 24580
  14.7 25.6 %copy-start.6 = (f32[3,2048]{1,0:T(4,128)S(1)}, f32[3,2048]{1,0:T(4,128)}, u32[]{:S(2)}) copy-start(f32[3,2048]{1,0:T(4,128)} %param.14) | copy-start | bytes 73732
  14.7 25.6 %copy-start.7 = (f32[3,2048]{1,0:T(4,128)S(1)}, f32[3,2048]{1,0:T(4,128)}, u32[]{:S(2)}) copy-start(f32[3,2048]{1,0:T(4,128)} %param.13) | copy-start | bytes 73732
  14.7 25.6 %copy-start.11 = (f32[2048]{0:T(1024)S(1)}, f32[2048]{0:T(1024)}, u32[]{:S(2)}) copy-start(f32[2048]{0:T(1024)} %param.15) | copy-start | bytes 24580
  49.6 18.6 %copy-start.5 = (s32[2048]{0:T(1024)S(1)}, s32[2048]{0:T(1024)}, u32[]{:S(2)}) copy-start(s32[2048]{0:T(1024)} %param.17) | copy-start | bytes 24580
  49.6 19.2 %copy-start.10 = (f32[2,2048]{1,0:T(2,128)S(1)}, f32[2,2048]{1,0:T(2,128)}, u32[]{:S(2)}) copy-start(f32[2,2048]{1,0:T(2,128)} %param.18) | copy-start | bytes 49156
  57.9 11.2 %copy-start.4 = (f32[27,256]{1,0:T(8,128)S(1)}, f32[27,256]{1,0:T(8,128)}, u32[]{:S(2)}) copy-start(f32[27,256]{1,0:T(8,128)} %param.19) | copy-start | bytes 82948
  60.9 23.1 %all-to-all-start = ((f32[8,512,8]{1,0,2:T(8,128)}), f32[8,512,8]{1,0,2:T(8,128)S(1)}, u32[]{:S(2)}, u32[]{:S(2)}) async-start(f32[8,512,8]{1,0,2:T(8,128)} %pad_maximum_fusion), calls=%async_computation | async-start | bytes 262144 | tf_op jit(solution)/shard_map/all_to_all | solution.py:102
  82.0 0.8 copy-start.3
  82.0 1.1 copy-start.2
  99.5 1.6 copy-start.1
  103.1 12.9 %all-to-all-start.1 = ((f32[3,512,8]{1,0,2:T(4,128)}), f32[3,512,8]{1,0,2:T(4,128)S(1)}, u32[]{:S(2)}, u32[]{:S(2)}) async-start(f32[3,512,8]{1,0,2:T(4,128)} %copy.158), calls=%async_computation.2 | async-start | bytes 131072 | tf_op jit(solution)/shard_map/all_to_all | solution.py:107
  109.1 7.7 %copy-start.9 = (s32[2048]{0:T(1024)S(1)}, s32[2048]{0:T(1024)}, u32[]{:S(2)}) copy-start(s32[2048]{0:T(1024)} %get-tuple-element.51) | copy-start | bytes 24580
  109.1 55.0 %reduce-scatter.5.cloned.1.call-start = ((), (), s32[]{:S(2)}) async-start(), calls=%async_computation.5 | async-start | bytes 655360 | tf_op jit(solution)/shard_map/reduce_scatter | solution.py:124
  116.8 9.1 %copy-start.8 = (f32[2048]{0:T(1024)S(1)}, f32[2048]{0:T(1024)}, u32[]{:S(2)}) copy-start(f32[2048]{0:T(1024)} %multiply_add_fusion.5) | copy-start | bytes 24580
  139.4 50.2 %reduce-scatter.3.cloned.1.call-start = ((), (), s32[]{:S(2)}) async-start(), calls=%async_computation.4 | async-start | bytes 1310720 | tf_op jit(solution)/shard_map/reduce_scatter | solution.py:123
Sparse Core Ops, SparseCore 0:
  139.6 18.4 reduce-scatter.4
  164.2 25.4 reduce-scatter.2
where the time goes:
time: 199 us; the launch traced here: 198 us
  local copies, waits for them, and re-layouts  80.6 us (41%)
  other arithmetic  52.5 us (26%)
  waiting for transfers between devices  29.9 us (15%)
  between operations  14.7 us (7%)
  starting transfers between devices  13.4 us (7%)
  blocking collectives  7.37 us (4%)
    scatter-add x2, other arithmetic, add_columns(): jnp.zeros((columns, values.shape[0]), jnp.float32).at[index]  35.7 us
    gather x4, local copies, waits for them, and re-layouts, take_columns(): return jnp.transpose(jnp.transpose(source)[index])  25.4 us
    reduce_scatter x1, waiting for transfers between devices, per_device(): lax.psum_scatter(partial_value, 'leaf', scatter_dimension=1, tiled=True)  24 us
    scatter x2, local copies, waits for them, and re-layouts, pack(): buffer = jnp.full((width, values.shape[0]), filler, jnp.float32).at[slot]...  14.2 us
    gather x1, local copies, waits for them, and re-layouts, per_device(): sorted_dest = dest[order]  11.8 us
    scatter x1, local copies, waits for them, and re-layouts, per_device(): jnp.zeros((count,), jnp.int32).at[order]  8.05 us
    all_gather x1, blocking collectives, per_device(): piece = lax.all_gather(patch_ctrl, 'leaf', axis=1, tiled=True)  7.37 us
    all_to_all x1, starting transfers between devices, per_device(): lax.all_to_all(payload, 'flow', split_axis=2, concat_axis=2, tiled=True)  7.28 us
  transfers between devices with their start and end apart: 4, of which 2 were waited for; matrix products, arithmetic and copies ran while one was open for 18% of the time, Pallas kernels for 0%

commit v1 on v0

--- a/solution.py
+++ b/solution.py
@@ -104,7 +104,19 @@
     speed = sample_flow(vel_coef, index, solid_weights(flat[1:4]))
     force = BETA * flat[7][None, :] * (flat[4:7] - speed) * valid[None, :].astype(jnp.float32)
     force = force.reshape(3, block.shape[1], block.shape[2])
-    back = lax.all_to_all(force, "flow", split_axis=2, concat_axis=2, tiled=True)
+    ways, here = (lax.axis_size("flow"), lax.axis_index("flow"))
+    width_2 = force.shape[2] // ways
+    lengths = list(force.shape)
+    lengths[2] = width_2
+    height = lengths[2]
+    lengths[2] = height * ways
+    full = jnp.zeros(lengths, force.dtype)
+    for mask in range(ways):
+        part = lax.dynamic_slice_in_dim(force, (here ^ mask) * width_2, width_2, axis=2)
+        if mask:
+            part = lax.ppermute(part, "flow", [(d, d ^ mask) for d in range(ways)])
+        full = lax.dynamic_update_slice_in_dim(full, part, (here ^ mask) * height, axis=2)
+    back = full
     result = (back, force, block)
     back, arrived, kept = result
     fsi = take_columns(back.reshape(3, width), slot)

time: 199 us -> 273 us (1.37)
  local copies, waits for them, and re-layouts: 80.6 us -> 149 us
  starting transfers between devices: 13.4 us -> 19.1 us
  waiting for transfers between devices: 29.9 us -> 26.2 us
    dynamic_update_slice x0 -> x8, local copies, waits for them, and re-layouts: none -> 47.3 us  [per_device(): lax.dynamic_update_slice_in_dim(full, part, (here ^ mask) * height, axis=2)]
    dynamic_slice x0 -> x9, local copies, waits for them, and re-layouts: none -> 13.3 us  [per_device(): lax.dynamic_slice_in_dim(force, (here ^ mask) * width_2, width_2, axis=2)]
    ppermute x0 -> x7, starting transfers between devices: none -> 11.7 us  [per_device(): part = lax.ppermute(part, 'flow', [(d, d ^ mask) for d in range(ways)])]
    all_to_all x1 -> x0, starting transfers between devices: 5.99 us -> none  [per_device(): lax.all_to_all(force, 'flow', split_axis=2, concat_axis=2, tiled=True)]
    all_to_all x1 -> x0, waiting for transfers between devices: 5.81 us -> none  [per_device(): lax.all_to_all(force, 'flow', split_axis=2, concat_axis=2, tiled=True)]
    ppermute x0 -> x7, local copies, waits for them, and re-layouts: none -> 4.44 us  [per_device(): part = lax.ppermute(part, 'flow', [(d, d ^ mask) for d in range(ways)])]
    unnamed x30 -> x57, local copies, waits for them, and re-layouts: 4.14 us -> 6.09 us
  transfers between devices with their start and end apart: 4 -> 10, of which waited for: 2 -> 1; matrix products, arithmetic and copies ran while one was open for 18% -> 32% of each run, Pallas kernels for 0% -> 0%
where the time goes in v1:
time: 273 us; the launch traced here: 272 us
  local copies, waits for them, and re-layouts  149 us (55%)
  other arithmetic  55.1 us (20%)
  waiting for transfers between devices  26.2 us (10%)
  starting transfers between devices  19.1 us (7%)
  between operations  15 us (5%)
  blocking collectives  7.19 us (3%)
    dynamic_update_slice x8, local copies, waits for them, and re-layouts, per_device(): lax.dynamic_update_slice_in_dim(full, part, (here ^ mask) * height, axis=2)  47.3 us
    scatter-add x2, other arithmetic, add_columns(): jnp.zeros((columns, values.shape[0]), jnp.float32).at[index]  35.8 us
    gather x4, local copies, waits for them, and re-layouts, take_columns(): return jnp.transpose(jnp.transpose(source)[index])  27.3 us
    reduce_scatter x1, waiting for transfers between devices, per_device(): lax.psum_scatter(partial_value, 'leaf', scatter_dimension=1, tiled=True)  26.1 us
    scatter x2, local copies, waits for them, and re-layouts, pack(): buffer = jnp.full((width, values.shape[0]), filler, jnp.float32).at[slot]...  14.2 us
    dynamic_slice x9, local copies, waits for them, and re-layouts, per_device(): lax.dynamic_slice_in_dim(force, (here ^ mask) * width_2, width_2, axis=2)  13.3 us
    gather x1, local copies, waits for them, and re-layouts, per_device(): sorted_dest = dest[order]  11.8 us
    ppermute x7, starting transfers between devices, per_device(): part = lax.ppermute(part, 'flow', [(d, d ^ mask) for d in range(ways)])  11.7 us
  transfers between devices with their start and end apart: 10, of which 1 were waited for; matrix products, arithmetic and copies ran while one was open for 32% of the time, Pallas kernels for 0%

profile of v1, /device:TPU:0, one launch (start us, length us, event | category | flops | bytes accessed | tf_op | source)
XLA Modules:
  0.0 272.0 jit_solution(68092845069776136)
XLA Ops:
  7.2 0.9 convert_reduce_fusion
  9.6 5.7 %sort.17 = (s32[2048]{0:T(1024)}, s32[2048]{0:T(1024)S(1)}) sort(s32[2048]{0:T(1024)} %bitcast.44, s32[2048]{0:T(1024)S(1)} %iota.11), dimensions={0}, to_apply=%region_0.0 | sort | flops 22528 | bytes 32768 | tf_op jit(solution)/shard_map/jit(argsort)/sort | solution.py:79
  15.4 11.8 %gather_fusion = s32[2048]{0:T(1024)S(1)} fusion(s32[2048]{0:T(1024)S(1)} %bitcast.45, s32[2048]{0:T(1024)S(1)} %get-tuple-element.64), kind=kCustom, calls=%fused_computation | custom fusion | bytes 24576 | tf_op jit(solution)/shard_map/gather | solution.py:80
  27.3 4.4 %compare_select_fusion.2 = s32[2048,1]{0,1:T(1,128)S(1)} fusion(s32[]{:T(128)} %bitcast.5, s32[]{:T(128)} %bitcast.6, s32[]{:T(128)} %bitcast.7, s32[]{:T(128)} %bitcast.8, s32[]{:T(128)} %bitcast.9, s32[]{:T(128)} %bitcast.11, s32[]{:T(128)} %bitcast.10, s32[2048,1]{0,1:T(1,128)S(1)} %bitcast.57), kind=kLoop, calls=%fused_computation.42 | loop fusion | flops 30720 | bytes 16412 | tf_op jit(solution)/shard_map/gather | solution.py:85
  32.3 8.0 %scatter_custom_fusion = s32[2048]{0:T(1024)S(1)} fusion(s32[2048]{0:T(1024)S(1)} %get-tuple-element.65, s32[2048]{0:T(1024)S(1)} %fusion.20, s32[]{:T(128)} %constant.23.clone.1), kind=kCustom, calls=%fused_computation.97 | custom fusion | bytes 8196 | tf_op jit(solution)/shard_map/scatter | solution.py:86
  41.3 6.1 %scatter_custom_fusion.1 = f32[4096,8]{1,0:T(8,128)S(1)} fusion(s32[2048]{0:T(1024)S(1)} %get-tuple-element.63, f32[2048,8]{1,0:T(8,128)S(1)} %copy.211, f32[]{:T(128)} %constant.22.clone.1), kind=kCustom, calls=%fused_computation.13 | custom fusion | bytes 131076 | tf_op jit(solution)/shard_map/scatter | solution.py:92
  48.1 2.0 slice_bitcast_fusion
  50.0 8.1 %scatter_custom_fusion.2 = f32[4096]{0:T(1024)S(1)} fusion(s32[2048]{0:T(1024)S(1)} %get-tuple-element.63, f32[2048]{0:T(1024)S(1)} %broadcast.365, f32[]{:T(128)} %constant.22.clone.1), kind=kCustom, calls=%fused_computation.86 | custom fusion | bytes 16388 | tf_op jit(solution)/shard_map/scatter | solution.py:92
  58.3 2.2 copy.213
  61.5 7.3 %all-to-all-start = ((f32[8,512,8]{1,0,2:T(8,128)}), f32[8,512,8]{1,0,2:T(8,128)S(1)}, u32[]{:S(2)}, u32[]{:S(2)}) async-start(f32[8,512,8]{1,0,2:T(8,128)} %pad_maximum_fusion), calls=%async_computation | async-start | bytes 262144 | tf_op jit(solution)/shard_map/all_to_all | solution.py:102
  69.8 7.2 %all_gather.3 = f32[27,1024]{0,1:T(8,128)S(1)} all-gather(f32[27,256]{0,1:T(8,128)S(1)} %copy.226), channel_id=1, replica_groups=mesh['flow'=8,'leaf'=4] {'leaf'}, dimensions={1}, use_global_device_ids=true | all-gather | bytes 138240 | tf_op jit(solution)/shard_map/all_gather | solution.py:125
  77.0 5.5 %gather_fusion.2 = f32[2048,27]{1,0:T(8,128)S(1)} fusion(f32[1024,27]{1,0:T(8,128)S(1)} %bitcast.47, s32[2048]{0:T(1024)S(1)} %get-tuple-element.61), kind=kCustom, calls=%fused_computation.2 | custom fusion | bytes 450560 | tf_op jit(solution)/shard_map/gather | solution.py:41
  85.6 0.9 copy.229
  88.9 1.0 mul.473
  89.9 1.2 copy.251
  91.1 12.7 %gather_fusion.1 = f32[4096,81]{1,0:T(8,128)S(1)} fusion(f32[2048,81]{1,0:T(8,128)S(1)} %bitcast.46, s32[4096]{0:T(1024)} %broadcast_clamp_fusion), kind=kCustom, calls=%fused_computation.1 | custom fusion | bytes 2670592 | tf_op jit(solution)/shard_map/gather | solution.py:41
  103.8 1.7 copy.220
  105.6 1.6 reshape.456
  107.2 0.9 multiply_reduce_fusion
  108.0 1.3 reduce_sum.42
  109.5 3.8 %constant_dynamic-slice_fusion = (f32[3,512,1]{2,1,0:T(8,128)}, f32[3,512,1]{2,1,0:T(8,128)}, f32[3,512,1]{2,1,0:T(8,128)}, f32[3,512,1]{2,1,0:T(8,128)S(1)}, f3...) fusion(f32[3,512,8]{2,1,0:T(8,128)S(1)} %multiply_multiply_fusion, ...), kind=kLoop, calls=%fused_computation.99 | loop fusion | bytes 98336 | tf_op jit(solution)/shard_map/dynamic_slice | solution.py:115
  113.2 1.4 copy.233
  114.6 1.4 copy.231
  116.0 2.0 collective-permute-start
  118.0 1.5 collective-permute-start.1
  120.5 1.4 copy.243
  121.9 1.4 copy.241
  124.2 2.8 %collective-permute-start.3 = (f32[3,512,1]{1,2,0:T(1,128)S(1)}, f32[3,512,1]{1,2,0:T(1,128)}, u32[]{:S(2)}, u32[]{:S(2)}) collective-permute-start(f32[3,512,1]{1,2,0:T(1,128)S(1)} %copy.237), channel_id=1, source_target_pairs={{0,16},{4,20},{8,24},{12,28},{16,0},{20,4},{24,8},{28,12},{1,17},{... | collective-permute-start | bytes 18440 | tf_op jit(solution)/shard_map/ppermute | solution.py:117
  127.1 1.5 collective-permute-start.4
  128.5 3.3 %collective-permute-start.5 = (f32[3,512,1]{1,2,0:T(1,128)S(1)}, f32[3,512,1]{1,2,0:T(1,128)}, u32[]{:S(2)}, u32[]{:S(2)}) collective-permute-start(f32[3,512,1]{1,2,0:T(1,128)S(1)} %copy.241), channel_id=1, source_target_pairs={{0,24},{4,28},{8,16},{12,20},{16,8},{20,12},{24,0},{28,4},{1,25},{... | collective-permute-start | bytes 18440 | tf_op jit(solution)/shard_map/ppermute | solution.py:117
  133.1 3.1 %copy.230 = f32[3,512,1]{0,2,1:T(1,128)S(1)} copy(f32[3,512,1]{2,1,0:T(8,128)S(1)} %copy-done.4) | data formatting | bytes 12288 | tf_op jit(solution)/shard_map/dynamic_slice | solution.py:115
  136.3 5.9 %dynamic_update_slice.24 = f32[3,512,8]{0,2,1:T(8,128)S(1)} dynamic-update-slice(f32[3,512,8]{0,2,1:T(8,128)S(1)} %broadcast_in_dim.75, f32[3,512,1]{0,2,1:T(1,128)S(1)} %copy.230, s32[]{:T(128)} %constant.23.clone.1, s32[]{:T(128)} %constant.23.clone.1, s32[]{:T(128)S(6)} %select_n.82) | dynamic-update-slice | bytes 12292 | tf_op jit(solution)/shard_map/dynamic_update_slice | solution.py:118
  142.4 5.9 %dynamic_update_slice.25 = f32[3,512,8]{0,2,1:T(8,128)S(1)} dynamic-update-slice(f32[3,512,8]{0,2,1:T(8,128)S(1)} %dynamic_update_slice.24, f32[3,512,1]{0,2,1:T(1,128)S(1)} %copy.232, s32[]{:T(128)} %constant.23.clone.1, s32[]{:T(128)} %constant.23.clone.1, s32[]{:T(128)S(6)} %select_n.83) | dynamic-update-slice | bytes 12292 | tf_op jit(solution)/shard_map/dynamic_update_slice | solution.py:118
  148.5 5.9 %dynamic_update_slice.26 = f32[3,512,8]{0,2,1:T(8,128)S(1)} dynamic-update-slice(f32[3,512,8]{0,2,1:T(8,128)S(1)} %dynamic_update_slice.25, f32[3,512,1]{0,2,1:T(1,128)S(1)} %copy.234, s32[]{:T(128)} %constant.23.clone.1, s32[]{:T(128)} %constant.23.clone.1, s32[]{:T(128)S(6)} %select_n.84) | dynamic-update-slice | bytes 12292 | tf_op jit(solution)/shard_map/dynamic_update_slice | solution.py:118
  154.4 0.8 copy.236
  155.2 6.1 %dynamic_update_slice.27 = f32[3,512,8]{0,2,1:T(8,128)S(1)} dynamic-update-slice(f32[3,512,8]{0,2,1:T(8,128)S(1)} %dynamic_update_slice.26, f32[3,512,1]{0,2,1:T(1,128)S(1)} %copy.236, s32[]{:T(128)} %constant.23.clone.1, s32[]{:T(128)} %constant.23.clone.1, s32[]{:T(128)S(6)} %select_n.85) | dynamic-update-slice | bytes 12292 | tf_op jit(solution)/shard_map/dynamic_update_slice | solution.py:118
  162.2 5.9 %dynamic_update_slice.28 = f32[3,512,8]{0,2,1:T(8,128)S(1)} dynamic-update-slice(f32[3,512,8]{0,2,1:T(8,128)S(1)} %dynamic_update_slice.27, f32[3,512,1]{0,2,1:T(1,128)S(1)} %copy.238, s32[]{:T(128)} %constant.23.clone.1, s32[]{:T(128)} %constant.23.clone.1, s32[]{:T(128)S(6)} %select_n.86) | dynamic-update-slice | bytes 12292 | tf_op jit(solution)/shard_map/dynamic_update_slice | solution.py:118
  168.9 5.9 %dynamic_update_slice.29 = f32[3,512,8]{0,2,1:T(8,128)S(1)} dynamic-update-slice(f32[3,512,8]{0,2,1:T(8,128)S(1)} %dynamic_update_slice.28, f32[3,512,1]{0,2,1:T(1,128)S(1)} %copy.240, s32[]{:T(128)} %constant.23.clone.1, s32[]{:T(128)} %constant.23.clone.1, s32[]{:T(128)S(6)} %select_n.87) | dynamic-update-slice | bytes 12292 | tf_op jit(solution)/shard_map/dynamic_update_slice | solution.py:118
  175.7 5.9 %dynamic_update_slice.30 = f32[3,512,8]{0,2,1:T(8,128)S(1)} dynamic-update-slice(f32[3,512,8]{0,2,1:T(8,128)S(1)} %dynamic_update_slice.29, f32[3,512,1]{0,2,1:T(1,128)S(1)} %copy.242, s32[]{:T(128)} %constant.23.clone.1, s32[]{:T(128)} %constant.23.clone.1, s32[]{:T(128)S(6)} %select_n.88) | dynamic-update-slice | bytes 12292 | tf_op jit(solution)/shard_map/dynamic_update_slice | solution.py:118
  182.4 5.9 %dynamic_update_slice.31 = f32[3,512,8]{0,2,1:T(8,128)S(1)} dynamic-update-slice(f32[3,512,8]{0,2,1:T(8,128)S(1)} %dynamic_update_slice.30, f32[3,512,1]{0,2,1:T(1,128)S(1)} %copy.244, s32[]{:T(128)} %constant.23.clone.1, s32[]{:T(128)} %constant.23.clone.1, s32[]{:T(128)S(6)} %select_n.89) | dynamic-update-slice | bytes 12292 | tf_op jit(solution)/shard_map/dynamic_update_slice | solution.py:118
  188.3 7.6 %gather_fusion.3 = f32[2048,3]{1,0:T(8,128)} fusion(f32[4096,3]{1,0:T(8,128)S(1)} %bitcast.48, s32[2048]{0:T(1024)S(1)} %copy-done.19), kind=kCustom, calls=%fused_computation.3 | custom fusion | bytes 57344 | tf_op jit(solution)/shard_map/gather | solution.py:41
  195.9 1.6 copy.245
  198.6 12.4 %scatter_custom_fusion.4 = f32[1024,27]{1,0:T(8,128)} fusion(s32[2048]{0:T(1024)} %get-tuple-element.60, f32[2048,27]{1,0:T(8,128)S(1)} %copy.246, f32[]{:T(128)} %constant.22.clone.1), kind=kCustom, calls=%fused_computation.22 | custom fusion | flops 55296 | bytes 111104 | tf_op jit(solution)/shard_map/scatter-add | solution.py:46
  211.3 0.8 copy.225
  212.2 23.5 %scatter_custom_fusion.3 = f32[2048,81]{1,0:T(8,128)} fusion(s32[4096]{0:T(1024)} %bitcast.59, f32[4096,81]{1,0:T(8,128)S(1)} %copy.225, f32[]{:T(128)} %constant.22.clone.1), kind=kCustom, calls=%fused_computation.17 | custom fusion | flops 331776 | bytes 664064 | tf_op jit(solution)/shard_map/scatter-add | solution.py:46
  235.7 1.6 copy.248
  237.3 26.1 %reduce-scatter.3.cloned.1.call-done = f32[81,512]{0,1:T(8,128)} async-done(((f32[81,2048]{0,1:T(8,128)}), f32[81,512]{0,1:T(8,128)}) %reduce-scatter.3.cloned.1.call-update) | async-done | bytes 165904 | tf_op jit(solution)/shard_map/reduce_scatter | solution.py:135
  263.4 1.8 copy.247
  (146 shorter events, 19.7 us)
Async XLA Ops:
  7.2 8.2 %copy-start = (s32[2048,1]{0,1:T(1,128)S(1)}, s32[2048,1]{0,1:T(1,128)}, u32[]{:S(2)}) copy-start(s32[2048,1]{0,1:T(1,128)} %param.11) | copy-start | bytes 24580
  15.4 25.6 %copy-start.17 = (f32[3,2048]{1,0:T(4,128)S(1)}, f32[3,2048]{1,0:T(4,128)}, u32[]{:S(2)}) copy-start(f32[3,2048]{1,0:T(4,128)} %param.14) | copy-start | bytes 73732
  15.4 25.6 %copy-start.18 = (f32[3,2048]{1,0:T(4,128)S(1)}, f32[3,2048]{1,0:T(4,128)}, u32[]{:S(2)}) copy-start(f32[3,2048]{1,0:T(4,128)} %param.13) | copy-start | bytes 73732
  15.4 25.6 %copy-start.21 = (f32[2048]{0:T(1024)S(1)}, f32[2048]{0:T(1024)}, u32[]{:S(2)}) copy-start(f32[2048]{0:T(1024)} %param.15) | copy-start | bytes 24580
  58.3 10.6 %copy-start.15 = (s32[2048]{0:T(1024)S(1)}, s32[2048]{0:T(1024)}, u32[]{:S(2)}) copy-start(s32[2048]{0:T(1024)} %param.17) | copy-start | bytes 24580
  58.3 11.2 %copy-start.20 = (f32[2,2048]{1,0:T(2,128)S(1)}, f32[2,2048]{1,0:T(2,128)}, u32[]{:S(2)}) copy-start(f32[2,2048]{1,0:T(2,128)} %param.18) | copy-start | bytes 49156
  58.3 11.4 %copy-start.14 = (f32[27,256]{1,0:T(8,128)S(1)}, f32[27,256]{1,0:T(8,128)}, u32[]{:S(2)}) copy-start(f32[27,256]{1,0:T(8,128)} %param.19) | copy-start | bytes 82948
  61.5 23.2 %all-to-all-start = ((f32[8,512,8]{1,0,2:T(8,128)}), f32[8,512,8]{1,0,2:T(8,128)S(1)}, u32[]{:S(2)}, u32[]{:S(2)}) async-start(f32[8,512,8]{1,0,2:T(8,128)} %pad_maximum_fusion), calls=%async_computation | async-start | bytes 262144 | tf_op jit(solution)/shard_map/all_to_all | solution.py:102
  68.8 166.9 %reduce-scatter.5.cloned.1.call-start = ((), (), s32[]{:S(2)}) async-start(), calls=%async_computation.4 | async-start | bytes 655360 | tf_op jit(solution)/shard_map/reduce_scatter | solution.py:136
  82.5 1.1 copy-start.6
  82.9 1.2 copy-start.10
  84.1 4.7 %copy-start.8 = (f32[3,2048]{1,0:T(4,128)}, f32[3,2048]{1,0:T(4,128)S(1)}, u32[]{:S(2)}) copy-start(f32[3,2048]{1,0:T(4,128)S(1)} %multiply_reduce_fusion.1) | copy-start | bytes 73732
  86.8 1.7 copy-start.13
  105.6 1.6 copy-start.2
  107.1 2.2 copy-start.1
  107.2 2.2 copy-start.5
  109.5 10.0 %copy-start.16 = (f32[2048]{0:T(1024)S(1)}, f32[2048]{0:T(1024)}, u32[]{:S(2)}) copy-start(f32[2048]{0:T(1024)} %multiply_reduce_fusion.2) | copy-start | bytes 24580
  113.2 6.7 %copy-start.12 = (f32[1,512,8]{1,2,0:T(8,128)S(1)}, f32[1,512,8]{1,2,0:T(8,128)}, u32[]{:S(2)}) copy-start(f32[1,512,8]{1,2,0:T(8,128)} %get-tuple-element.48) | copy-start | bytes 49156
  116.0 12.5 %collective-permute-start = (f32[3,512,1]{1,2,0:T(1,128)S(1)}, f32[3,512,1]{1,2,0:T(1,128)S(1)}, u32[]{:S(2)}, u32[]{:S(2)}) collective-permute-start(f32[3,512,1]{1,2,0:T(1,128)S(1)} %copy.231), channel_id=1, source_target_pairs={{0,4},{4,0},{8,12},{12,8},{16,20},{20,16},{24,28},{28,24},{1,5},{5... | collective-permute-start | bytes 18440 | tf_op jit(solution)/shard_map/ppermute | solution.py:117
  118.0 13.8 %collective-permute-start.1 = (f32[3,512,1]{1,2,0:T(1,128)S(1)}, f32[3,512,1]{1,2,0:T(1,128)S(1)}, u32[]{:S(2)}, u32[]{:S(2)}) collective-permute-start(f32[3,512,1]{1,2,0:T(1,128)S(1)} %copy.233), channel_id=1, source_target_pairs={{0,8},{4,12},{8,0},{12,4},{16,24},{20,28},{24,16},{28,20},{1,9},{5... | collective-permute-start | bytes 18440 | tf_op jit(solution)/shard_map/ppermute | solution.py:117
  119.9 3.4 %copy-start.3 = (f32[3,512,1]{2,1,0:T(8,128)S(1)}, f32[3,512,1]{2,1,0:T(8,128)}, u32[]{:S(2)}) copy-start(f32[3,512,1]{2,1,0:T(8,128)} %get-tuple-element.30) | copy-start | bytes 18436
  120.3 12.7 %copy-start.7 = (f32[3,4096]{1,0:T(4,128)S(1)}, f32[3,4096]{1,0:T(4,128)}, u32[]{:S(2)}) copy-start(f32[3,4096]{1,0:T(4,128)} %multiply_reduce_fusion) | copy-start | bytes 147460
  123.6 9.5 %copy-start.4 = (f32[3,512,1]{2,1,0:T(8,128)S(1)}, f32[3,512,1]{2,1,0:T(8,128)}, u32[]{:S(2)}) copy-start(f32[3,512,1]{2,1,0:T(8,128)} %get-tuple-element.35) | copy-start | bytes 18436
  124.1 30.2 %collective-permute-start.2 = (f32[3,512,1]{1,2,0:T(1,128)S(1)}, f32[3,512,1]{1,2,0:T(1,128)}, u32[]{:S(2)}, u32[]{:S(2)}) collective-permute-start(f32[3,512,1]{1,2,0:T(1,128)S(1)} %copy.235), channel_id=1, source_target_pairs={{0,12},{4,8},{8,4},{12,0},{16,28},{20,24},{24,20},{28,16},{1,13},{... | collective-permute-start | bytes 18440 | tf_op jit(solution)/shard_map/ppermute | solution.py:117
  124.2 37.1 %collective-permute-start.3 = (f32[3,512,1]{1,2,0:T(1,128)S(1)}, f32[3,512,1]{1,2,0:T(1,128)}, u32[]{:S(2)}, u32[]{:S(2)}) collective-permute-start(f32[3,512,1]{1,2,0:T(1,128)S(1)} %copy.237), channel_id=1, source_target_pairs={{0,16},{4,20},{8,24},{12,28},{16,0},{20,4},{24,8},{28,12},{1,17},{... | collective-permute-start | bytes 18440 | tf_op jit(solution)/shard_map/ppermute | solution.py:117
  127.1 41.0 %collective-permute-start.4 = (f32[3,512,1]{1,2,0:T(1,128)S(1)}, f32[3,512,1]{1,2,0:T(1,128)}, u32[]{:S(2)}, u32[]{:S(2)}) collective-permute-start(f32[3,512,1]{1,2,0:T(1,128)S(1)} %copy.239), channel_id=1, source_target_pairs={{0,20},{4,16},{8,28},{12,24},{16,4},{20,0},{24,12},{28,8},{1,21},{... | collective-permute-start | bytes 18440 | tf_op jit(solution)/shard_map/ppermute | solution.py:117
  128.5 3.3 %copy-start.24 = (f32[3,512,1]{1,2,0:T(1,128)}, f32[3,512,1]{1,2,0:T(1,128)S(1)}, u32[]{:S(2)}) copy-start(f32[3,512,1]{1,2,0:T(1,128)S(1)} %collective-permute-done) | copy-start | bytes 18436
  128.5 46.3 %collective-permute-start.5 = (f32[3,512,1]{1,2,0:T(1,128)S(1)}, f32[3,512,1]{1,2,0:T(1,128)}, u32[]{:S(2)}, u32[]{:S(2)}) collective-permute-start(f32[3,512,1]{1,2,0:T(1,128)S(1)} %copy.241), channel_id=1, source_target_pairs={{0,24},{4,28},{8,16},{12,20},{16,8},{20,12},{24,0},{28,4},{1,25},{... | collective-permute-start | bytes 18440 | tf_op jit(solution)/shard_map/ppermute | solution.py:117
  131.8 0.6 copy-start.22
  132.4 49.1 %collective-permute-start.6 = (f32[3,512,1]{1,2,0:T(1,128)S(1)}, f32[3,512,1]{1,2,0:T(1,128)}, u32[]{:S(2)}, u32[]{:S(2)}) collective-permute-start(f32[3,512,1]{1,2,0:T(1,128)S(1)} %copy.243), channel_id=1, source_target_pairs={{0,28},{4,24},{8,20},{12,16},{16,12},{20,8},{24,4},{28,0},{1,29},{... | collective-permute-start | bytes 18440 | tf_op jit(solution)/shard_map/ppermute | solution.py:117
  133.0 9.2 %copy-start.25 = (f32[3,512,1]{1,2,0:T(1,128)S(1)}, f32[3,512,1]{1,2,0:T(1,128)}, u32[]{:S(2)}) copy-start(f32[3,512,1]{1,2,0:T(1,128)} %copy-done.24) | copy-start | bytes 18436
  133.1 15.2 %copy-start.23 = (f32[3,512,1]{1,2,0:T(1,128)S(1)}, f32[3,512,1]{1,2,0:T(1,128)}, u32[]{:S(2)}) copy-start(f32[3,512,1]{1,2,0:T(1,128)} %copy-done.22) | copy-start | bytes 18436
  154.3 33.9 %copy-start.19 = (s32[2048]{0:T(1024)S(1)}, s32[2048]{0:T(1024)}, u32[]{:S(2)}) copy-start(s32[2048]{0:T(1024)} %get-tuple-element.62) | copy-start | bytes 24580
  188.3 9.2 %copy-start.9 = (f32[3,2048]{1,0:T(4,128)S(1)}, f32[3,2048]{1,0:T(4,128)}, u32[]{:S(2)}) copy-start(f32[3,2048]{1,0:T(4,128)} %copy-done.8) | copy-start | bytes 73732
  188.3 9.2 %copy-start.11 = (f32[3,2048]{1,0:T(4,128)S(1)}, f32[3,2048]{1,0:T(4,128)}, u32[]{:S(2)}) copy-start(f32[3,2048]{1,0:T(4,128)} %param.16) | copy-start | bytes 73732
  211.0 52.4 %reduce-scatter.3.cloned.1.call-start = ((), (), s32[]{:S(2)}) async-start(), calls=%async_computation.3 | async-start | bytes 1310720 | tf_op jit(solution)/shard_map/reduce_scatter | solution.py:135
Sparse Core Ops, SparseCore 0:
  211.1 21.8 reduce-scatter.4
  235.8 27.5 reduce-scatter.2
